TPU v7x, 32 devices: a whole 2x2x4 slice. The times are simulated.
32 devices in a mesh: tp: 8 (over y, x, core), col: 4 (over z).
Axes of the slice: x: 2, y: 2, z: 4, core: 2. Of those that a mesh axis runs over, the one named last changes fastest.
Arguments:
- gate_in: bfloat16 [128, 53248], P('col', 'tp'), may hold values from -6 to 6
- up_in: bfloat16 [128, 53248], P('col', 'tp'), may hold values from -6 to 6
- down_weight: bfloat16 [53248, 16384], P('tp', 'col'), may hold values from -0.02734375 to 0.02734375
- residual: bfloat16 [128, 16384], P('tp', 'col'), may hold values from -30 to 30
- norm_gain: bfloat16 [16384], P('col'), may hold values from 0.5 to 1.5
Outputs:
- stream: bfloat16 [128, 16384], P('tp', 'col')
- normed: bfloat16 [128, 16384], P('tp', 'col')
All inputs are finite; a program needn't handle non-finite values.
Results may differ from a plain program's by a relative error of at most 0.0034.
Values may be sent and summed in bfloat16 or wider, within the bound.
A program may use at most 128 MiB of HBM per device.

v0:
```python
import jax
import jax.numpy as jnp
from jax import lax
from jax.sharding import PartitionSpec as P

D = 16384


def gated(gate_part, up_part):
    return (jax.nn.silu(gate_part.astype(jnp.float32)) * up_part.astype(jnp.float32)).astype(
        jnp.bfloat16
    )


def body(gate_in, up_in, down_weight, residual, norm_gain):
    local_act = gated(gate_in, up_in)
    hidden = lax.all_gather(local_act, "col", axis=0, tiled=True)
    partial_value = jnp.dot(hidden, down_weight, preferred_element_type=jnp.float32)
    branch = lax.psum_scatter(partial_value, "tp", scatter_dimension=0, tiled=True)
    summed = residual.astype(jnp.float32) + branch
    local_squares = jnp.sum(summed * summed, axis=1, keepdims=True)
    mean_square = lax.psum(local_squares, "col") / D
    scaled = summed * lax.rsqrt(mean_square + 1e-05) * norm_gain.astype(jnp.float32)[None, :]
    return (summed.astype(jnp.bfloat16), scaled.astype(jnp.bfloat16))


def solution(mesh):
    in_specs = (P("col", "tp"), P("col", "tp"), P("tp", "col"), P("tp", "col"), P("col"))
    out_specs = (P("tp", "col"), P("tp", "col"))
    return jax.shard_map(body, mesh=mesh, in_specs=in_specs, out_specs=out_specs, check_vma=False)
```

profile of v0, /device:TPU:0, one launch (start us, length us, event | category | flops | bytes accessed | tf_op | source)
XLA Modules:
  0.0 134.5 jit_solution(9100638335402482563)
XLA Ops:
  7.2 0.0 all-gather.2.cloned.1.call-start
  7.2 2.1 %fusion.4 = bf16[32,6656]{1,0:T(8,128)(2,1)} fusion(bf16[32,6656]{1,0:T(8,128)(2,1)} %param.6, bf16[32,6656]{1,0:T(8,128)(2,1)} %param.5), kind=kLoop, calls=%fused_computation.6 | loop fusion | flops 1703936 | bytes 1277952 | tf_op jit(solution)/shard_map/convert_element_type | solution.py:10
  9.4 0.0 all-gather.2.cloned.1.call-update
  9.4 0.0 reduce-scatter.2.cloned.1.call-start
  9.4 42.0 %all-gather.2.cloned.1.call-done = bf16[128,6656]{1,0:T(8,128)(2,1)} async-done(((bf16[32,6656]{1,0:T(8,128)(2,1)}), bf16[128,6656]{1,0:T(8,128)(2,1)}) %all-gather.2.cloned.1.call-update) | async-done | bytes 1703952 | tf_op jit(solution)/shard_map/all_gather | solution.py:17
  51.5 21.5 %fusion.6 = f32[128,4096]{1,0:T(8,128)} fusion(bf16[128,6656]{1,0:T(8,128)(2,1)} %all-gather.2.cloned.1.call-done, bf16[6656,4096]{1,0:T(8,128)(2,1)} %param.7), kind=kOutput, calls=%fused_computation.12 | convolution fusion | flops 6979321856 | bytes 58327040 | tf_op jit(solution)/shard_map/dot_general | solution.py:18
  73.0 0.0 copy-start.1
  73.0 0.0 copy-start
  73.0 0.0 reduce-scatter.2.cloned.1.call-update
  73.0 0.7 copy-done.1
  73.7 39.4 %reduce-scatter.2.cloned.1.call-done = f32[16,4096]{1,0:T(8,128)} async-done(((f32[128,4096]{1,0:T(8,128)}), f32[16,4096]{1,0:T(8,128)}) %reduce-scatter.2.cloned.1.call-update) | async-done | bytes 262160 | tf_op jit(solution)/shard_map/reduce_scatter | solution.py:19
  113.1 0.0 copy-done
  113.1 1.1 multiply_reduce_fusion
  114.2 11.7 %psum.7 = f32[16,1]{0,1:T(1,128)S(1)} all-reduce(f32[16,1]{0,1:T(1,128)S(1)} %bitcast.5), channel_id=1, replica_groups=mesh['tp'=8,'col'=4] {'col'}, use_global_device_ids=true, to_apply=%region_2.3 | all-reduce | flops 16 | bytes 128 | tf_op jit(solution)/shard_map/psum | solution.py:22
  125.9 1.7 %multiply_convert_fusion = (bf16[16,4096]{1,0:T(8,128)(2,1)}, bf16[16,4096]{1,0:T(8,128)(2,1)}) fusion(f32[4096]{0:T(1024)S(1)} %convert_element_type.26, f32[16]{0:T(128)S(1)} %rsqrt_bitcast_fusion, f32[16,4096]{1,0:T(8,128)} %reduce-scatter.2.cloned.1.call-done, bf16[16,4096]{1,0:T(8,128)(2,1)S(1)} %copy-done), kind=kLoop, calls=%fused_computation.7 | loop fusion | flops 393216 | bytes 671808 | tf_op jit(solution)/shard_map/convert_element_type | solution.py:24
  (2 shorter events, 0.0 us)
Async XLA Ops:
  7.2 44.3 %all-gather.2.cloned.1.call-start = ((), (), s32[]{:S(2)}) async-start(), calls=%async_computation.1 | async-start | bytes 2129920 | tf_op jit(solution)/shard_map/all_gather | solution.py:17
  9.4 103.7 %reduce-scatter.2.cloned.1.call-start = ((), (), s32[]{:S(2)}) async-start(), calls=%async_computation.2 | async-start | bytes 2359296 | tf_op jit(solution)/shard_map/reduce_scatter | solution.py:19
  73.0 0.7 copy-start.1
  73.0 40.1 %copy-start = (bf16[16,4096]{1,0:T(8,128)(2,1)S(1)}, bf16[16,4096]{1,0:T(8,128)(2,1)}, u32[]{:S(2)}) copy-start(bf16[16,4096]{1,0:T(8,128)(2,1)} %param.8) | copy-start | bytes 393220
Sparse Core Ops, SparseCore 0:
  9.5 41.8 all-gather.1
  73.1 39.9 reduce-scatter.1
where the time goes:
time: 135 us; the launch traced here: 134 us
  waiting for transfers between devices  81.5 us (60%)
  matrix products  21.5 us (16%)
  between operations  14 us (10%)
  blocking collectives  11.7 us (9%)
  other arithmetic  4.96 us (4%)
    all_gather x1, waiting for transfers between devices, body(): hidden = lax.all_gather(local_act, 'col', axis=0, tiled=True)  42 us
    reduce_scatter x1, waiting for transfers between devices, body(): lax.psum_scatter(partial_value, 'tp', scatter_dimension=0, tiled=True)  39.4 us
    dot_general x1, matrix products, body(): jnp.dot(hidden, down_weight, preferred_element_type=jnp.float32)  21.5 us
    psum x1, blocking collectives, body(): mean_square = lax.psum(local_squares, 'col') / D  11.7 us
  transfers between devices with their start and end apart: 2, of which 2 were waited for; matrix products, arithmetic and copies ran while one was open for 0% of the time, Pallas kernels for 0%

commit v1 on v0

--- a/solution.py
+++ b/solution.py
@@ -4,6 +4,16 @@
 from jax.sharding import PartitionSpec as P
 
 D = 16384
+
+
+def pass_along(x, name, d):
+    count = lax.axis_size(name)
+    current, parts = (x, [x])
+    for _ in range(count - 1):
+        current = lax.ppermute(current, name, [(i, (i + 1) % count) for i in range(count)])
+        parts.insert(0, current)
+    line = jnp.concatenate(parts, axis=d)
+    return jnp.roll(line, (lax.axis_index(name) + 1) * x.shape[d], axis=d)
 
 
 def gated(gate_part, up_part):
@@ -14,7 +24,7 @@
 
 def body(gate_in, up_in, down_weight, residual, norm_gain):
     local_act = gated(gate_in, up_in)
-    hidden = lax.all_gather(local_act, "col", axis=0, tiled=True)
+    hidden = pass_along(local_act, "col", 0)
     partial_value = jnp.dot(hidden, down_weight, preferred_element_type=jnp.float32)
     branch = lax.psum_scatter(partial_value, "tp", scatter_dimension=0, tiled=True)
     summed = residual.astype(jnp.float32) + branch

time: 135 us -> 130 us (0.963)
  waiting for transfers between devices: 81.5 us -> 75.6 us
  starting transfers between devices: 0.08 us -> 3.15 us
    all_gather x1 -> x0, waiting for transfers between devices: 42 us -> none  [body(): hidden = lax.all_gather(local_act, 'col', axis=0, tiled=True)]
    ppermute x0 -> x3, waiting for transfers between devices: none -> 36.5 us  [pass_along(): lax.ppermute(current, name, [(i, (i + 1) % count) for i in range(count)])]
    ppermute x0 -> x3, starting transfers between devices: none -> 3.11 us  [pass_along(): lax.ppermute(current, name, [(i, (i + 1) % count) for i in range(count)])]
  transfers between devices with their start and end apart: 2 -> 4, of which waited for: 2 -> 4; matrix products, arithmetic and copies ran while one was open for 0% -> 0% of each run, Pallas kernels for 0% -> 0%
where the time goes in v1:
time: 130 us; the launch traced here: 129 us
  waiting for transfers between devices  75.6 us (58%)
  matrix products  20.5 us (16%)
  between operations  14.1 us (11%)
  blocking collectives  11.7 us (9%)
  other arithmetic  4.19 us (3%)
  starting transfers between devices  3.15 us (2%)
    reduce_scatter x1, waiting for transfers between devices, body(): lax.psum_scatter(partial_value, 'tp', scatter_dimension=0, tiled=True)  39 us
    ppermute x3, waiting for transfers between devices, pass_along(): lax.ppermute(current, name, [(i, (i + 1) % count) for i in range(count)])  36.5 us
    dot_general x1, matrix products, body(): jnp.dot(hidden, down_weight, preferred_element_type=jnp.float32)  20.5 us
    psum x1, blocking collectives, body(): mean_square = lax.psum(local_squares, 'col') / D  11.7 us
    ppermute x3, starting transfers between devices, pass_along(): lax.ppermute(current, name, [(i, (i + 1) % count) for i in range(count)])  3.11 us
  transfers between devices with their start and end apart: 4, of which 4 were waited for; matrix products, arithmetic and copies ran while one was open for 0% of the time, Pallas kernels for 0%

profile of v1, /device:TPU:0, one launch (start us, length us, event | category | flops | bytes accessed | tf_op | source)
XLA Modules:
  0.0 129.5 jit_solution(12645149262315582291)
XLA Ops:
  7.2 0.0 reduce-scatter.2.cloned.1.call-start
  7.2 1.4 %fusion.6 = bf16[32,6656]{1,0:T(8,128)(2,1)S(1)} fusion(bf16[32,6656]{1,0:T(8,128)(2,1)} %param.6, bf16[32,6656]{1,0:T(8,128)(2,1)} %param.5), kind=kLoop, calls=%fused_computation.8 | loop fusion | flops 1703936 | bytes 1277952 | tf_op jit(solution)/shard_map/convert_element_type | solution.py:20
  8.6 3.1 %collective-permute-start = (bf16[32,6656]{1,0:T(8,128)(2,1)S(1)}, bf16[32,6656]{1,0:T(8,128)(2,1)S(1)}, u32[]{:S(2)}, u32[]{:S(2)}) collective-permute-start(bf16[32,6656]{1,0:T(8,128)(2,1)S(1)} %fusion.6), channel_id=1, source_target_pairs={{0,1},{1,2},{2,3},{3,0},{4,5},{5,6},{6,7},{7,4},{8,9},{9,10},{10,1... | collective-permute-start | bytes 1277960 | tf_op jit(solution)/shard_map/ppermute | solution.py:13
  11.7 11.8 %collective-permute-done = bf16[32,6656]{1,0:T(8,128)(2,1)S(1)} collective-permute-done((bf16[32,6656]{1,0:T(8,128)(2,1)S(1)}, bf16[32,6656]{1,0:T(8,128)(2,1)S(1)}, u32[]{:S(2)}, u32[]{:S(2)}) %collective-permute-start) | collective-permute-done | bytes 426016 | tf_op jit(solution)/shard_map/ppermute | solution.py:13
  23.5 0.0 collective-permute-start.1
  23.5 12.8 %collective-permute-done.1 = bf16[32,6656]{1,0:T(8,128)(2,1)S(1)} collective-permute-done((bf16[32,6656]{1,0:T(8,128)(2,1)S(1)}, bf16[32,6656]{1,0:T(8,128)(2,1)S(1)}, u32[]{:S(2)}, u32[]{:S(2)}) %collective-permute-start.1) | collective-permute-done | bytes 426016 | tf_op jit(solution)/shard_map/ppermute | solution.py:13
  36.3 0.0 collective-permute-start.2
  36.3 11.9 %collective-permute-done.2 = bf16[32,6656]{1,0:T(8,128)(2,1)S(1)} collective-permute-done((bf16[32,6656]{1,0:T(8,128)(2,1)S(1)}, bf16[32,6656]{1,0:T(8,128)(2,1)S(1)}, u32[]{:S(2)}, u32[]{:S(2)}) %collective-permute-start.2) | collective-permute-done | bytes 426016 | tf_op jit(solution)/shard_map/ppermute | solution.py:13
  48.5 0.0 copy-start.1
  48.6 0.0 copy-start
  48.6 20.5 %fusion = f32[128,4096]{1,0:T(8,128)} fusion(bf16[6656,4096]{1,0:T(8,128)(2,1)} %param.7, bf16[256,6656]{1,0:T(8,128)(2,1)S(1)} %constant_dynamic-update-slice_fusion, s32[]{:T(128)S(6)} %select_n.14), kind=kOutput, calls=%fused_computation | convolution fusion | flops 6979321856 | bytes 58327044 | tf_op jit(solution)/shard_map/dot_general | solution.py:28
  69.1 0.0 reduce-scatter.2.cloned.1.call-update
  69.1 0.0 copy-done.1
  69.1 39.0 %reduce-scatter.2.cloned.1.call-done = f32[16,4096]{1,0:T(8,128)} async-done(((f32[128,4096]{1,0:T(8,128)}), f32[16,4096]{1,0:T(8,128)}) %reduce-scatter.2.cloned.1.call-update) | async-done | bytes 262160 | tf_op jit(solution)/shard_map/reduce_scatter | solution.py:29
  108.1 0.0 copy-done
  108.1 1.1 multiply_reduce_fusion
  109.2 11.7 %psum.7 = f32[16,1]{0,1:T(1,128)S(1)} all-reduce(f32[16,1]{0,1:T(1,128)S(1)} %bitcast.4), channel_id=1, replica_groups=mesh['tp'=8,'col'=4] {'col'}, use_global_device_ids=true, to_apply=%region_2.3 | all-reduce | flops 16 | bytes 128 | tf_op jit(solution)/shard_map/psum | solution.py:32
  120.9 1.7 %multiply_convert_fusion = (bf16[16,4096]{1,0:T(8,128)(2,1)}, bf16[16,4096]{1,0:T(8,128)(2,1)}) fusion(f32[4096]{0:T(1024)S(1)} %convert_element_type.26, f32[16]{0:T(128)S(1)} %rsqrt_bitcast_fusion, f32[16,4096]{1,0:T(8,128)} %reduce-scatter.2.cloned.1.call-done, bf16[16,4096]{1,0:T(8,128)(2,1)S(1)} %copy-done), kind=kLoop, calls=%fused_computation.9 | loop fusion | flops 393216 | bytes 671808 | tf_op jit(solution)/shard_map/convert_element_type | solution.py:34
  (10 shorter events, 0.3 us)
Async XLA Ops:
  7.2 101.0 %reduce-scatter.2.cloned.1.call-start = ((), (), s32[]{:S(2)}) async-start(), calls=%async_computation.1 | async-start | bytes 2359296 | tf_op jit(solution)/shard_map/reduce_scatter | solution.py:29
  8.6 14.9 %collective-permute-start = (bf16[32,6656]{1,0:T(8,128)(2,1)S(1)}, bf16[32,6656]{1,0:T(8,128)(2,1)S(1)}, u32[]{:S(2)}, u32[]{:S(2)}) collective-permute-start(bf16[32,6656]{1,0:T(8,128)(2,1)S(1)} %fusion.6), channel_id=1, source_target_pairs={{0,1},{1,2},{2,3},{3,0},{4,5},{5,6},{6,7},{7,4},{8,9},{9,10},{10,1... | collective-permute-start | bytes 1277960 | tf_op jit(solution)/shard_map/ppermute | solution.py:13
  23.5 12.8 %collective-permute-start.1 = (bf16[32,6656]{1,0:T(8,128)(2,1)S(1)}, bf16[32,6656]{1,0:T(8,128)(2,1)S(1)}, u32[]{:S(2)}, u32[]{:S(2)}) collective-permute-start(bf16[32,6656]{1,0:T(8,128)(2,1)S(1)} %collective-permute-done), channel_id=1, source_target_pairs={{0,1},{1,2},{2,3},{3,0},{4,5},{5,6},{6,7},{7,4},{8,9},{9,10},{10,1... | collective-permute-start | bytes 1277960 | tf_op jit(solution)/shard_map/ppermute | solution.py:13
  36.3 11.9 %collective-permute-start.2 = (bf16[32,6656]{1,0:T(8,128)(2,1)S(1)}, bf16[32,6656]{1,0:T(8,128)(2,1)S(1)}, u32[]{:S(2)}, u32[]{:S(2)}) collective-permute-start(bf16[32,6656]{1,0:T(8,128)(2,1)S(1)} %collective-permute-done.1), channel_id=1, source_target_pairs={{0,1},{1,2},{2,3},{3,0},{4,5},{5,6},{6,7},{7,4},{8,9},{9,10},{10,1... | collective-permute-start | bytes 1277960 | tf_op jit(solution)/shard_map/ppermute | solution.py:13
  48.5 20.6 %copy-start.1 = (bf16[4096]{0:T(1024)(128)(2,1)S(1)}, bf16[4096]{0:T(1024)(128)(2,1)}, u32[]{:S(2)}) copy-start(bf16[4096]{0:T(1024)(128)(2,1)} %param.9) | copy-start | bytes 24580
  48.6 59.6 %copy-start = (bf16[16,4096]{1,0:T(8,128)(2,1)S(1)}, bf16[16,4096]{1,0:T(8,128)(2,1)}, u32[]{:S(2)}) copy-start(bf16[16,4096]{1,0:T(8,128)(2,1)} %param.8) | copy-start | bytes 393220
Sparse Core Ops, SparseCore 0:
  69.2 38.8 reduce-scatter.1
